TPU v7x, 32 devices: a whole 2x2x4 slice. The times are simulated.
32 devices in a mesh: dp: 8 (over y, x, core), tensor: 4 (over z).
Axes of the slice: x: 2, y: 2, z: 4, core: 2. Of those that a mesh axis runs over, the one named last changes fastest.
Arguments:
- text: bfloat16 [8, 256, 5120], P('dp', None, 'tensor'), may hold values from -6 to 6
- prompts: bfloat16 [8, 100, 5120], P('dp', None, 'tensor'), may hold values from -6 to 6
- gain: float32 [5120], replicated, may hold values from 0.1 to 1.9
- w_query: bfloat16 [5120, 3072], P(None, 'tensor'), may hold values from -0.069877124 to 0.069877124, as said below
- w_key: bfloat16 [5120, 3072], P(None, 'tensor'), may hold values from -1.2577882 to 1.2577882, as said below
- w_value: bfloat16 [5120, 3072], P(None, 'tensor'), may hold values from -0.078125 to 0.078125
- cotangent: bfloat16 [8, 356, 3072], P('dp', None, 'tensor'), may hold values from -6 to 6
- task_of: int32 [8], replicated, may hold values from 0 to 7, as said below
- lengths: int32 [8], replicated, may hold values from 1 to 256, as said below
- slot: int32 [8], replicated, may hold values from 0 to 7, as said below
Outputs:
- attn_out: bfloat16 [8, 356, 3072], P('dp', None, 'tensor')
- prompt_grad: float32 [8, 100, 5120], P('dp', None, 'tensor')
Inputs may be any that keep to these rules, and one draw needn't show every extreme that they name: `task_of`: nondecreasing along the source order. `lengths`: some example has exactly 256 text tokens; rows of an example beyond its length are padding. `slot`: a permutation of 0 to 7; position s lies on index s // 1 of dp. `w_query`: entries of order 5120 ** -0.5. `w_key`: entries of order 5120 ** -0.5 or larger.
All inputs are finite; a program needn't handle non-finite values.
Results may differ from a plain program's by a relative error of at most 0.0082.
Values may be sent and summed in bfloat16 or wider, within the bound.
A program may use at most 128 MiB of HBM per device.

v0:
```python
import math

import jax
import jax.numpy as jnp
from jax import lax
from jax.sharding import PartitionSpec as P

HD = 128


def rope_tables(row_count):
    half_dim = HD // 2
    frequency = 10000.0 ** (-jnp.arange(half_dim, dtype=jnp.float32) / half_dim)
    angle_table = jnp.arange(row_count, dtype=jnp.float32)[:, None] * frequency[None, :]
    return (jnp.cos(angle_table), jnp.sin(angle_table))


def rotate(vectors, cosine_table, sine_table):
    half_dim = vectors.shape[-1] // 2
    first_half = vectors[..., :half_dim]
    second_half = vectors[..., half_dim:]
    cosine_b = cosine_table[:, None, :]
    sine_b = sine_table[:, None, :]
    return jnp.concatenate(
        [
            first_half * cosine_b - second_half * sine_b,
            second_half * cosine_b + first_half * sine_b,
        ],
        axis=-1,
    )


def unrotate(vectors, cosine_table, sine_table):
    half_dim = vectors.shape[-1] // 2
    first_half = vectors[..., :half_dim]
    second_half = vectors[..., half_dim:]
    cosine_b = cosine_table[:, None, :]
    sine_b = sine_table[:, None, :]
    return jnp.concatenate(
        [
            first_half * cosine_b + second_half * sine_b,
            second_half * cosine_b - first_half * sine_b,
        ],
        axis=-1,
    )


def transpose_product(grad_low, matrix):
    return lax.dot_general(
        grad_low, matrix, (((1,), (1,)), ((), ())), preferred_element_type=jnp.float32
    )


def attention_window(full_rows, gain, w_query, w_key, w_value, cotangent, valid_rows, prompt_len):
    batch_size, row_count, model_width = full_rows.shape
    head_count = w_query.shape[1] // HD
    wide_rows = full_rows.astype(jnp.float32)
    inv_rms = lax.rsqrt(jnp.mean(wide_rows * wide_rows, axis=-1) + 1e-05)
    normed = (
        (wide_rows * inv_rms[..., None] * gain)
        .astype(jnp.bfloat16)
        .reshape(batch_size * row_count, model_width)
    )
    cosine_table, sine_table = rope_tables(row_count)

    def project(matrix):
        return jnp.dot(normed, matrix, preferred_element_type=jnp.float32).reshape(
            batch_size, row_count, head_count, HD
        )

    queries = rotate(project(w_query), cosine_table, sine_table).astype(jnp.bfloat16)
    key_rows = rotate(project(w_key), cosine_table, sine_table).astype(jnp.bfloat16)
    value_rows = project(w_value).astype(jnp.bfloat16)
    score_scale = 1.0 / math.sqrt(HD)
    scores = (
        jnp.einsum("erhd,ekhd->ehrk", queries, key_rows, preferred_element_type=jnp.float32)
        * score_scale
    )
    rows_at = jnp.arange(row_count, dtype=jnp.int32)
    row_limit = prompt_len + valid_rows
    allowed = (rows_at[None, None, :] <= rows_at[None, :, None]) & (
        rows_at[None, None, :] < row_limit[:, None, None]
    )
    allowed = allowed[:, None]
    scores = jnp.where(allowed, scores, -1e30)
    row_peak = jnp.max(scores, axis=-1, keepdims=True)
    weights = jnp.where(allowed, jnp.exp(scores - row_peak), 0.0)
    probability = weights / jnp.sum(weights, axis=-1, keepdims=True)
    probs_low = probability.astype(jnp.bfloat16)
    live_rows = rows_at[None, :] < row_limit[:, None]
    mixed_rows = jnp.einsum(
        "ehrk,ekhd->erhd", probs_low, value_rows, preferred_element_type=jnp.float32
    )
    mixed_rows = jnp.where(live_rows[:, :, None, None], mixed_rows, 0.0)
    output = mixed_rows.reshape(batch_size, row_count, head_count * HD).astype(jnp.bfloat16)
    upstream = jnp.where(
        live_rows[:, :, None, None], cotangent.reshape(batch_size, row_count, head_count, HD), 0.0
    )
    grad_prob = jnp.einsum(
        "erhd,ekhd->ehrk", upstream, value_rows, preferred_element_type=jnp.float32
    )
    row_delta = jnp.sum(probability * grad_prob, axis=-1, keepdims=True)
    grad_score = (probability * (grad_prob - row_delta)).astype(jnp.bfloat16)
    grad_query = (
        jnp.einsum(
            "ehrk,ekhd->erhd",
            grad_score[:, :, :prompt_len, :],
            key_rows,
            preferred_element_type=jnp.float32,
        )
        * score_scale
    )
    grad_key = (
        jnp.einsum(
            "ehrk,erhd->ekhd",
            grad_score[:, :, :, :prompt_len],
            queries,
            preferred_element_type=jnp.float32,
        )
        * score_scale
    )
    grad_value = jnp.einsum(
        "ehrk,erhd->ekhd",
        probs_low[:, :, :, :prompt_len],
        upstream,
        preferred_element_type=jnp.float32,
    )
    cosine_lead = cosine_table[:prompt_len]
    sine_lead = sine_table[:prompt_len]
    flat_rows = batch_size * prompt_len
    grad_query = (
        unrotate(grad_query, cosine_lead, sine_lead)
        .astype(jnp.bfloat16)
        .reshape(flat_rows, head_count * HD)
    )
    grad_key = (
        unrotate(grad_key, cosine_lead, sine_lead)
        .astype(jnp.bfloat16)
        .reshape(flat_rows, head_count * HD)
    )
    grad_value = grad_value.astype(jnp.bfloat16).reshape(flat_rows, head_count * HD)
    grad_normed = (
        transpose_product(grad_query, w_query)
        + transpose_product(grad_key, w_key)
        + transpose_product(grad_value, w_value)
    )
    grad_normed = grad_normed.reshape(batch_size, prompt_len, model_width) * gain
    prompt_rows = wide_rows[:, :prompt_len]
    prompt_inv = inv_rms[:, :prompt_len, None]
    grad_rows = prompt_inv * grad_normed - prompt_rows * prompt_inv**3 * jnp.mean(
        grad_normed * prompt_rows, axis=-1, keepdims=True
    )
    return (output, grad_rows)


def on_device(text, prompts, gain, w_query, w_key, w_value, cotangent, task_of, lengths, slot):
    dp_count = lax.axis_size("dp")
    my_index = lax.axis_index("dp")
    ex_dev = text.shape[0]
    task_dev = prompts.shape[0]
    prompt_len = prompts.shape[1]
    example_count = slot.shape[0]
    task_count = task_dev * dp_count
    places = jnp.arange(example_count, dtype=jnp.int32)
    matching = slot[None, :] == places[:, None]
    task_slot = jnp.sum(jnp.where(matching, task_of[None, :], 0), axis=1)
    length_slot = jnp.sum(jnp.where(matching, lengths[None, :], 0), axis=1)
    first_place = my_index * ex_dev
    my_lengths = lax.dynamic_slice_in_dim(length_slot, first_place, ex_dev)
    task_ids = jnp.arange(task_count, dtype=jnp.int32)
    spread_text, spread_prompts = (
        lax.all_to_all(text, "dp", split_axis=2, concat_axis=0, tiled=True),
        lax.all_to_all(prompts, "dp", split_axis=2, concat_axis=0, tiled=True),
    )
    taking = matching.astype(jnp.bfloat16)
    placed_text = jnp.einsum(
        "se,erc->src", taking, spread_text, preferred_element_type=jnp.bfloat16
    )
    choosing = (task_slot[:, None] == task_ids[None, :]).astype(jnp.bfloat16)
    placed_prompts = jnp.einsum(
        "st,tpc->spc", choosing, spread_prompts, preferred_element_type=jnp.bfloat16
    )
    placed = jnp.concatenate([placed_prompts, placed_text], axis=1)
    placed = placed.reshape(dp_count, ex_dev, placed.shape[1], placed.shape[2])
    local_rows = lax.all_to_all(placed, "dp", split_axis=0, concat_axis=3, tiled=True)[0]
    full_rows = lax.all_gather(local_rows, "tensor", axis=2, tiled=True)
    output, grad_part = attention_window(
        full_rows, gain, w_query, w_key, w_value, cotangent, my_lengths, prompt_len
    )
    grad_share = lax.psum_scatter(grad_part, "tensor", scatter_dimension=2, tiled=True)
    spread_grads = lax.all_to_all(grad_share, "dp", split_axis=2, concat_axis=0, tiled=True)
    collecting = (task_ids[:, None] == task_slot[None, :]).astype(jnp.float32)
    per_task = jnp.einsum("ts,spc->tpc", collecting, spread_grads, precision=lax.Precision.HIGHEST)
    prompt_grad = lax.all_to_all(per_task, "dp", split_axis=0, concat_axis=2, tiled=True)
    return (output, prompt_grad)


def solution(mesh):
    in_specs = (
        P("dp", None, "tensor"),
        P("dp", None, "tensor"),
        P(),
        P(None, "tensor"),
        P(None, "tensor"),
        P(None, "tensor"),
        P("dp", None, "tensor"),
        P(),
        P(),
        P(),
    )
    out_specs = (P("dp", None, "tensor"), P("dp", None, "tensor"))
    return jax.shard_map(
        on_device, mesh=mesh, in_specs=in_specs, out_specs=out_specs, check_vma=False
    )
```

profile of v0, /device:TPU:11, one launch (start us, length us, event | category | flops | bytes accessed | tf_op | source)
XLA Modules:
  0.0 269.7 jit_solution(17136922004648161386)
XLA Ops:
  7.2 1.4 copy.42
  9.1 7.5 %reduce.9 = bf16[1280,100]{1,0:T(8,128)(2,1)S(1)} reduce(bf16[1280,1,100]{2,1,0:T(2,128)(2,1)S(1)} %bitcast.161, bf16[]{:T(256)} %broadcast.173), dimensions={1}, to_apply=%bitcast.131.reduce_sub_computation | reduce | bytes 512002
  17.9 4.5 %all-to-all-start = ((bf16[8,2,8000]{2,1,0:T(2,128)(2,1)}), bf16[8,2,8000]{2,1,0:T(2,128)(2,1)S(1)}, u32[]{:S(2)}, u32[]{:S(2)}) async-start(bf16[8,2,8000]{2,1,0:T(2,128)(2,1)} %reshape.364), calls=%async_computation | async-start | bytes 516096 | tf_op jit(solution)/shard_map/all_to_all | solution.py:173
  22.5 1.7 copy.44
  24.2 6.9 %reduce.8 = bf16[1280,256]{1,0:T(8,128)(2,1)S(1)} reduce(bf16[1280,1,256]{2,1,0:T(2,128)(2,1)S(1)} %bitcast.158, bf16[]{:T(256)} %broadcast.173), dimensions={1}, to_apply=%bitcast.129.reduce_sub_computation | reduce | bytes 1310722
  32.1 4.2 %all-to-all-start.1 = ((bf16[8,2,20480]{2,1,0:T(2,128)(2,1)}), bf16[8,2,20480]{2,1,0:T(2,128)(2,1)S(1)}, u32[]{:S(2)}, u32[]{:S(2)}) async-start(bf16[8,2,20480]{2,1,0:T(2,128)(2,1)} %reshape.362), calls=%async_computation.1 | async-start | bytes 1310720 | tf_op jit(solution)/shard_map/all_to_all | solution.py:172
  38.1 7.8 %all-to-all-done.1 = bf16[8,2,20480]{2,1,0:T(2,128)(2,1)S(1)} async-done(((bf16[8,2,20480]{2,1,0:T(2,128)(2,1)}), bf16[8,2,20480]{2,1,0:T(2,128)(2,1)S(1)}, u32[]{:S(2)}, u32[]{:S(2)}) %all-to-all-start.1) | async-done | bytes 655392 | tf_op jit(solution)/shard_map/all_to_all | solution.py:172
  47.8 16.9 %all_to_all.87 = bf16[8,1,356,160]{2,3,1,0:T(8,128)(2,1)S(1)} all-to-all(bf16[8,1,356,160]{2,3,1,0:T(8,128)(2,1)S(1)} %copy.46), channel_id=1, replica_groups=mesh['dp'=8,'tensor'=4] {'dp'}, dimensions={0} | all-to-all | bytes 1822720 | tf_op jit(solution)/shard_map/all_to_all | solution.py:185
  64.6 1.3 copy.47
  66.2 10.7 %copy.50 = bf16[5120,768]{0,1:T(8,128)(2,1)} copy(bf16[5120,768]{1,0:T(8,128)(2,1)} %param.14) | data formatting | bytes 15728640 | tf_op args[4]
  76.9 10.8 %copy.49 = bf16[5120,768]{0,1:T(8,128)(2,1)} copy(bf16[5120,768]{1,0:T(8,128)(2,1)} %param.13) | data formatting | bytes 15728640 | tf_op args[3]
  88.0 10.6 %copy.48 = bf16[5120,768]{0,1:T(8,128)(2,1)} copy(bf16[5120,768]{1,0:T(8,128)(2,1)} %param.15) | data formatting | bytes 15728640 | tf_op args[5]
  101.1 35.0 %all-gather.2.cloned.1.call-done = bf16[1,356,5120]{2,1,0:T(8,128)(2,1)} async-done(((bf16[1,356,1280]{2,1,0:T(8,128)(2,1)}), bf16[1,356,5120]{2,1,0:T(8,128)(2,1)}) %all-gather.2.cloned.1.call-update) | async-done | bytes 3645456 | tf_op jit(solution)/shard_map/all_gather | solution.py:186
  136.1 3.0 %multiply_reduce_fusion = f32[356]{0:T(512)S(1)} fusion(bf16[1,356,5120]{2,1,0:T(8,128)(2,1)} %all-gather.2.cloned.1.call-done), kind=kLoop, calls=%fused_computation.3 | loop fusion | flops 5467804 | bytes 3646864 | tf_op jit(solution)/shard_map/reduce_sum | solution.py:58
  139.2 6.9 %convolution_bitcast_fusion.1 = f32[1,356,6,128]{3,1,2,0:T(8,128)S(1)} fusion(bf16[6,128,5120]{2,1,0:T(8,128)(2,1)} %bitcast.157, f32[5120]{0:T(1024)S(1)} %copy-done.7, f32[356]{0:T(512)S(1)} %add_rsqrt_fusion, bf16[1,356,5120]{2,1,0:T(8,128)(2,1)S(1)} %copy-done), kind=kOutput, calls=%fused_computation.23 | convolution fusion | flops 2806988800 | bytes 12625296 | tf_op jit(solution)/shard_map/dot_general | solution.py:67
  146.2 3.3 %convolution_bitcast_fusion.2 = f32[1,356,6,128]{3,1,2,0:T(8,128)S(1)} fusion(bf16[6,128,5120]{2,1,0:T(8,128)(2,1)S(1)} %bitcast.156, f32[5120]{0:T(1024)S(1)} %copy-done.7, f32[356]{0:T(512)S(1)} %add_rsqrt_fusion, bf16[1,356,5120]{2,1,0:T(8,128)(2,1)S(1)} %copy-done), kind=kOutput, calls=%fused_computation.24 | convolution fusion | flops 2806988800 | bytes 12625296 | tf_op jit(solution)/shard_map/dot_general | solution.py:67
  150.3 3.8 %fusion.59 = (f32[6,356]{1,0:T(8,128)S(1)}, f32[6,356,356]{1,2,0:T(8,128)}) fusion(pred[356,356]{0,1:T(8,128)(4,1)S(1)} %fusion.32, bf16[356,6,64]{2,0,1:T(8,128)(2,1)S(1)} %get-tuple-element.16, bf16[356,6,64]{2,0,1:T(8,128)(2,1)S(1)} %get-tuple-element.17, bf16[356,6,64]{2,0,1:T(8,128)(2,1)S(1)} %get-tuple-element.9, ...), kind=kOutput, calls=%fused_computation.100 | convolution fusion | flops 200656192 | bytes 4270576 | tf_op jit(solution)/shard_map/sub | solution.py:87
  154.0 2.4 convert_bitcast_fusion
  157.1 6.6 %convolution_convert_fusion = bf16[356,6,128]{2,0,1:T(8,128)(2,1)S(1)} fusion(bf16[6,128,5120]{2,1,0:T(8,128)(2,1)} %bitcast.153, f32[5120]{0:T(1024)S(1)} %copy-done.7, f32[356]{0:T(512)S(1)} %add_rsqrt_fusion, bf16[1,356,5120]{2,1,0:T(8,128)(2,1)S(1)} %copy-done.1), kind=kOutput, calls=%fused_computation.25 | convolution fusion | flops 2807262208 | bytes 12078480 | tf_op jit(solution)/shard_map/dot_general | solution.py:67
  164.5 1.4 copy-done.2
  169.2 3.8 %fusion.60 = f32[100,5120]{1,0:T(8,128)} fusion(bf16[100,768]{1,0:T(8,128)(2,1)S(1)} %bitcast.177, bf16[5120,768]{1,0:T(8,128)(2,1)S(1)} %bitcast.150), kind=kOutput, calls=%fused_computation.101 | convolution fusion | flops 786432000 | bytes 10065920 | tf_op jit(solution)/shard_map/dot_general | solution.py:49
  173.3 4.3 %convolution_add_fusion.1 = f32[100,5120]{1,0:T(8,128)S(1)} fusion(f32[100,5120]{1,0:T(8,128)} %fusion.60, bf16[100,768]{1,0:T(8,128)(2,1)S(1)} %bitcast.176, bf16[5120,768]{1,0:T(8,128)(2,1)S(1)} %bitcast.152), kind=kOutput, calls=%fused_computation.6 | convolution fusion | flops 786944000 | bytes 12113920 | tf_op jit(solution)/shard_map/dot_general | solution.py:49
  178.5 2.7 %fusion.8 = (f32[100]{0:T(128)S(1)}, f32[100,5120]{1,0:T(8,128)S(1)}) fusion(f32[1,356,5120]{2,1,0:T(8,128)S(1)} %convert_element_type.77, f32[5120]{0:T(1024)S(1)} %copy-done.7, f32[100,5120]{1,0:T(8,128)S(1)} %convolution_add_fusion.1, bf16[100,768]{1,0:T(8,128)(2,1)S(1)} %bitcast.175, bf16[5120,768]{1,0:T(8,128)(2,1)S(1)} %bitcast.148), kind=kOutput, calls=%fused_computation.15 | convolution fusion | flops 788479872 | bytes 14182800 | tf_op jit(solution)/shard_map/dot_general | solution.py:49
  181.2 1.8 bitcast_subtract_fusion
  183.0 44.3 %reduce-scatter.2.cloned.1.call-done = f32[1,100,1280]{2,1,0:T(8,128)} async-done(((f32[1,100,5120]{2,1,0:T(8,128)}), f32[1,100,1280]{2,1,0:T(8,128)}) %reduce-scatter.2.cloned.1.call-update) | async-done | bytes 512016 | tf_op jit(solution)/shard_map/reduce_scatter | solution.py:190
  227.4 2.1 copy.60
  229.4 14.1 %all_to_all.88 = f32[1,100,1280]{1,0,2:T(1,128)S(1)} all-to-all(f32[1,100,1280]{1,0,2:T(1,128)} %copy.60), channel_id=1, replica_groups=mesh['dp'=8,'tensor'=4] {'dp'}, dimensions={2} | all-to-all | bytes 1024000 | tf_op jit(solution)/shard_map/all_to_all | solution.py:191
  245.2 5.9 %all-to-all-start.4 = ((f32[8,100,160]{1,2,0:T(8,128)}), f32[8,100,160]{1,2,0:T(8,128)}, u32[]{:S(2)}, u32[]{:S(2)}) async-start(f32[8,100,160]{1,2,0:T(8,128)} %copy.62), calls=%async_computation.5 | async-start | bytes 1310720 | tf_op jit(solution)/shard_map/all_to_all | solution.py:194
  251.1 2.8 %fusion.17 = bf16[1,356,6,128]{3,1,2,0:T(8,128)(2,1)} fusion(bf16[356,6,128]{2,0,1:T(8,128)(2,1)} %copy-done.6, pred[356]{0:T(512)(128)(4,1)S(1)} %copy-done.14, f32[6,356,356]{1,2,0:T(8,128)S(1)} %copy-done.3, f32[6,356]{1,0:T(8,128)S(1)} %copy-done.9), kind=kOutput, calls=%fused_computation.28 | convolution fusion | flops 196734144 | bytes 4144196 | tf_op jit(solution)/shard_map/ehrk,ekhd->erhd/dot_general | solution.py:91
  253.9 1.4 copy.52
  256.4 4.5 %all-to-all-done.4 = f32[8,100,160]{1,2,0:T(8,128)} async-done(((f32[8,100,160]{1,2,0:T(8,128)}), f32[8,100,160]{1,2,0:T(8,128)}, u32[]{:S(2)}, u32[]{:S(2)}) %all-to-all-start.4) | async-done | bytes 512032 | tf_op jit(solution)/shard_map/all_to_all | solution.py:194
  260.9 2.0 copy.64
  (104 shorter events, 18.3 us)
Async XLA Ops:
  7.2 15.3 %copy-start.4 = (bf16[1,256,1280]{2,1,0:T(8,128)(2,1)S(1)}, bf16[1,256,1280]{2,1,0:T(8,128)(2,1)}, u32[]{:S(2)}) copy-start(bf16[1,256,1280]{2,1,0:T(8,128)(2,1)} %param.10) | copy-start | bytes 1966084
  17.9 14.2 %all-to-all-start = ((bf16[8,2,8000]{2,1,0:T(2,128)(2,1)}), bf16[8,2,8000]{2,1,0:T(2,128)(2,1)S(1)}, u32[]{:S(2)}, u32[]{:S(2)}) async-start(bf16[8,2,8000]{2,1,0:T(2,128)(2,1)} %reshape.364), calls=%async_computation | async-start | bytes 516096 | tf_op jit(solution)/shard_map/all_to_all | solution.py:173
  22.4 13.9 %copy-start.12 = (s32[8]{0:T(128)S(1)}, s32[8]{0:T(128)}, u32[]{:S(2)}) copy-start(s32[8]{0:T(128)} %param.19) | copy-start | bytes 100
  22.4 13.9 %copy-start.15 = (s32[8]{0:T(128)S(1)}, s32[8]{0:T(128)}, u32[]{:S(2)}) copy-start(s32[8]{0:T(128)} %param.18) | copy-start | bytes 100
  22.4 13.9 %copy-start.16 = (s32[8]{0:T(128)S(1)}, s32[8]{0:T(128)}, u32[]{:S(2)}) copy-start(s32[8]{0:T(128)} %param.17) | copy-start | bytes 100
  32.1 13.8 %all-to-all-start.1 = ((bf16[8,2,20480]{2,1,0:T(2,128)(2,1)}), bf16[8,2,20480]{2,1,0:T(2,128)(2,1)S(1)}, u32[]{:S(2)}, u32[]{:S(2)}) async-start(bf16[8,2,20480]{2,1,0:T(2,128)(2,1)} %reshape.362), calls=%async_computation.1 | async-start | bytes 1310720 | tf_op jit(solution)/shard_map/all_to_all | solution.py:172
  36.3 99.8 %all-gather.2.cloned.1.call-start = ((), (), s32[]{:S(2)}) async-start(), calls=%async_computation.6 | async-start | bytes 4608000 | tf_op jit(solution)/shard_map/all_gather | solution.py:186
  36.5 1.7 copy-start.10
  66.0 161.4 %reduce-scatter.2.cloned.1.call-start = ((), (), s32[]{:S(2)}) async-start(), calls=%async_computation.7 | async-start | bytes 2662400 | tf_op jit(solution)/shard_map/reduce_scatter | solution.py:190
  76.9 10.8 %copy-start.5 = (bf16[1,356,768]{2,1,0:T(8,128)(2,1)S(1)}, bf16[1,356,768]{2,1,0:T(8,128)(2,1)}, u32[]{:S(2)}) copy-start(bf16[1,356,768]{2,1,0:T(8,128)(2,1)} %param.16) | copy-start | bytes 1640452
  98.6 40.5 %copy-start.7 = (f32[5120]{0:T(1024)S(1)}, f32[5120]{0:T(1024)}, u32[]{:S(2)}) copy-start(f32[5120]{0:T(1024)} %param.12) | copy-start | bytes 61444
  100.6 0.5 copy-start.13
  136.1 3.2 %copy-start = (bf16[1,356,5120]{2,1,0:T(8,128)(2,1)S(1)}, bf16[1,356,5120]{2,1,0:T(8,128)(2,1)}, u32[]{:S(2)}) copy-start(bf16[1,356,5120]{2,1,0:T(8,128)(2,1)} %all-gather.2.cloned.1.call-done) | copy-start | bytes 10936324
  136.1 10.1 %slice-start.6 = ((s8[7864320]{0:T(1024)(128)(4,1)}), s8[4194304]{0:T(1024)(128)(4,1)S(1)}, s32[]{:S(2)}) async-start(s8[7864320]{0:T(1024)(128)(4,1)} %bitcast.154), calls=%async_computation.14 | async-start | bytes 8388608
  139.2 6.9 %slice-start.7 = ((s8[7864320]{0:T(1024)(128)(4,1)}), s8[3670016]{0:T(1024)(128)(4,1)S(1)}, s32[]{:S(2)}) async-start(s8[7864320]{0:T(1024)(128)(4,1)} %bitcast.154), calls=%async_computation.15 | async-start | bytes 7340032
  154.0 10.5 %copy-start.8 = (f32[6,356]{1,0:T(8,128)}, f32[6,356]{1,0:T(8,128)S(1)}, u32[]{:S(2)}) copy-start(f32[6,356]{1,0:T(8,128)S(1)} %get-tuple-element.22) | copy-start | bytes 25636
  154.0 3.0 %copy-start.1 = (bf16[1,356,5120]{2,1,0:T(8,128)(2,1)S(1)}, bf16[1,356,5120]{2,1,0:T(8,128)(2,1)}, u32[]{:S(2)}) copy-start(bf16[1,356,5120]{2,1,0:T(8,128)(2,1)} %all-gather.2.cloned.1.call-done) | copy-start | bytes 10936324
  157.1 6.7 %copy-start.14 = (pred[356]{0:T(512)(128)(4,1)S(1)}, pred[356]{0:T(512)(128)(4,1)}, u32[]{:S(2)}) copy-start(pred[356]{0:T(512)(128)(4,1)} %copy-done.13) | copy-start | bytes 1072
  163.7 3.2 %copy-start.6 = (bf16[356,6,128]{2,0,1:T(8,128)(2,1)}, bf16[356,6,128]{2,0,1:T(8,128)(2,1)S(1)}, u32[]{:S(2)}) copy-start(bf16[356,6,128]{2,0,1:T(8,128)(2,1)S(1)} %convolution_convert_fusion) | copy-start | bytes 1640452
  163.7 2.1 copy-start.2
  163.7 5.5 %slice-start.2 = ((s8[7864320]{0:T(1024)(128)(4,1)}), s8[4194304]{0:T(1024)(128)(4,1)S(1)}, s32[]{:S(2)}) async-start(s8[7864320]{0:T(1024)(128)(4,1)} %bitcast.149), calls=%async_computation.10 | async-start | bytes 8388608
  165.9 3.4 %slice-start.3 = ((s8[7864320]{0:T(1024)(128)(4,1)}), s8[3670016]{0:T(1024)(128)(4,1)S(1)}, s32[]{:S(2)}) async-start(s8[7864320]{0:T(1024)(128)(4,1)} %bitcast.149), calls=%async_computation.11 | async-start | bytes 7340032
  168.5 4.7 %slice-start.4 = ((s8[7864320]{0:T(1024)(128)(4,1)}), s8[4194304]{0:T(1024)(128)(4,1)S(1)}, s32[]{:S(2)}) async-start(s8[7864320]{0:T(1024)(128)(4,1)} %bitcast.151), calls=%async_computation.12 | async-start | bytes 8388608
  169.2 4.0 %slice-start.5 = ((s8[7864320]{0:T(1024)(128)(4,1)}), s8[3670016]{0:T(1024)(128)(4,1)S(1)}, s32[]{:S(2)}) async-start(s8[7864320]{0:T(1024)(128)(4,1)} %bitcast.151), calls=%async_computation.13 | async-start | bytes 7340032
  173.2 5.2 %slice-start = ((s8[7864320]{0:T(1024)(128)(4,1)}), s8[4194304]{0:T(1024)(128)(4,1)S(1)}, s32[]{:S(2)}) async-start(s8[7864320]{0:T(1024)(128)(4,1)} %bitcast.147), calls=%async_computation.8 | async-start | bytes 8388608
  173.3 5.2 %slice-start.1 = ((s8[7864320]{0:T(1024)(128)(4,1)}), s8[3670016]{0:T(1024)(128)(4,1)S(1)}, s32[]{:S(2)}) async-start(s8[7864320]{0:T(1024)(128)(4,1)} %bitcast.147), calls=%async_computation.9 | async-start | bytes 7340032
  183.0 60.5 %copy-start.11 = (s32[8]{0:T(128)S(1)}, s32[8]{0:T(128)}, u32[]{:S(2)}) copy-start(s32[8]{0:T(128)} %copy-done.10) | copy-start | bytes 100
  183.0 68.1 %copy-start.3 = (f32[6,356,356]{1,2,0:T(8,128)S(1)}, f32[6,356,356]{1,2,0:T(8,128)}, u32[]{:S(2)}) copy-start(f32[6,356,356]{1,2,0:T(8,128)} %get-tuple-element.23) | copy-start | bytes 9124996
  183.0 68.1 %copy-start.9 = (f32[6,356]{1,0:T(8,128)S(1)}, f32[6,356]{1,0:T(8,128)}, u32[]{:S(2)}) copy-start(f32[6,356]{1,0:T(8,128)} %copy-done.8) | copy-start | bytes 25636
  245.2 15.6 %all-to-all-start.4 = ((f32[8,100,160]{1,2,0:T(8,128)}), f32[8,100,160]{1,2,0:T(8,128)}, u32[]{:S(2)}, u32[]{:S(2)}) async-start(f32[8,100,160]{1,2,0:T(8,128)} %copy.62), calls=%async_computation.5 | async-start | bytes 1310720 | tf_op jit(solution)/shard_map/all_to_all | solution.py:194
Sparse Core Ops, SparseCore 0:
  66.1 69.9 all-gather.1
  183.1 44.1 reduce-scatter.1
where the time goes:
time: 274 us; the launch traced here: 270 us
  waiting for transfers between devices  91.6 us (33%)
  local copies, waits for them, and re-layouts  53 us (19%)
  matrix products  37.9 us (14%)
  blocking collectives  31 us (11%)
  other arithmetic  26.2 us (10%)
  between operations  15.3 us (6%)
  starting transfers between devices  14.9 us (5%)
    unnamed x71, local copies, waits for them, and re-layouts  46.4 us
    reduce_scatter x1, waiting for transfers between devices, on_device(): lax.psum_scatter(grad_part, 'tensor', scatter_dimension=2, tiled=True)  44.3 us
    all_gather x1, waiting for transfers between devices, on_device(): full_rows = lax.all_gather(local_rows, 'tensor', axis=2, tiled=True)  35 us
    all_to_all x1, blocking collectives, on_device(): lax.all_to_all(placed, 'dp', split_axis=0, concat_axis=3, tiled=True)[0]  16.9 us
    dot_general x3, matrix products, project(): jnp.dot(normed, matrix, preferred_element_type=jnp.float32)  16.8 us
    unnamed x6, other arithmetic  14.3 us
    all_to_all x1, blocking collectives, on_device(): lax.all_to_all(grad_share, 'dp', split_axis=2, concat_axis=0, tiled=True)  14.1 us
    dot_general x3, matrix products, transpose_product(): lax.dot_general(grad_low, matrix, (((1,), (1,)), ((), ())), preferred_ele...  10.8 us
  transfers between devices with their start and end apart: 5, of which 4 were waited for; matrix products, arithmetic and copies ran while one was open for 19% of the time, Pallas kernels for 0%

commit v1 on v0

--- a/solution.py
+++ b/solution.py
@@ -1,8 +1,11 @@
+import functools
 import math
 
 import jax
 import jax.numpy as jnp
 from jax import lax
+from jax.experimental import pallas as pl
+from jax.experimental.pallas import tpu as pltpu
 from jax.sharding import PartitionSpec as P
 
 HD = 128
@@ -195,6 +198,418 @@
     return (output, prompt_grad)
 
 
+MESH = pl.DeviceIdType.MESH
+PAD_POS = 1 << 20
+
+
+def dispatch_kernel(source_ref, task_ref, inp_ref, out_ref, recv, send, sem1, sem2, semz):
+    n, m = lax.axis_size("dp"), lax.axis_size("tensor")
+    me, t = lax.axis_index("dp"), lax.axis_index("tensor")
+    right, left = lax.rem(t + 1, m), lax.rem(t + m - 1, m)
+    split = inp_ref.shape[1] * 2 // 3
+
+    barrier = pltpu.get_barrier_semaphore()
+    for k in range(1, n):
+        pl.semaphore_signal(
+            barrier, inc=1, device_id=(lax.rem(me + k, n), t), device_id_type=MESH
+        )
+    for z in (left, right):
+        pl.semaphore_signal(barrier, inc=1, device_id=(me, z), device_id_type=MESH)
+    pl.semaphore_wait(barrier, n + 1)
+
+    first = []
+    for k in range(1, n):
+        peer = lax.rem(me + k, n)
+        copy = pltpu.make_async_remote_copy(
+            src_ref=inp_ref.at[peer],
+            dst_ref=recv.at[me],
+            send_sem=sem1.at[0, k],
+            recv_sem=sem1.at[1, k],
+            device_id=(peer, t),
+            device_id_type=MESH,
+        )
+        copy.start()
+        first.append(copy)
+    recv[me] = inp_ref[me]
+    for copy in first:
+        copy.wait_recv()
+
+    second = []
+    for k in range(1, n):
+        peer = lax.rem(me + k, n)
+        send[k, :split] = recv[source_ref[peer], :split]
+        send[k, split:] = recv[task_ref[peer], split:]
+        copy = pltpu.make_async_remote_copy(
+            src_ref=send.at[k],
+            dst_ref=out_ref.at[t, me],
+            send_sem=sem2.at[0, k],
+            recv_sem=sem2.at[1, k],
+            device_id=(peer, t),
+            device_id_type=MESH,
+        )
+        copy.start()
+        second.append(copy)
+    out_ref[t, me, :split] = recv[source_ref[me], :split]
+    out_ref[t, me, split:] = recv[task_ref[me], split:]
+
+    def hop(origin, k, distance, way):
+        chunk = lax.rem(me + n - k, n)
+        place = out_ref.at[origin, chunk]
+        copy = pltpu.make_async_remote_copy(
+            src_ref=place,
+            dst_ref=place,
+            send_sem=semz.at[0, way, distance, k],
+            recv_sem=semz.at[1, way, distance, k],
+            device_id=(me, left if way else right),
+            device_id_type=MESH,
+        )
+        copy.start()
+        return copy
+
+    def reach(k, way):
+        half = m // 2
+        long_way = k % 2
+        return half if way == long_way else m - 1 - half
+
+    hops = {}
+    for k in range(n):
+        if k:
+            second[k - 1].wait_recv()
+        for way in (0, 1):
+            if reach(k, way) >= 1:
+                hops[way, 1, k] = hop(t, k, 1, way)
+    for distance in range(1, m // 2 + 1):
+        for k in range(n):
+            for way in (0, 1):
+                if distance <= reach(k, way):
+                    hops[way, distance, k].wait_recv()
+                    if distance < reach(k, way):
+                        origin = lax.rem(t + (m - distance if way == 0 else distance), m)
+                        hops[way, distance + 1, k] = hop(origin, k, distance + 1, way)
+    for copy in first + second:
+        copy.wait_send()
+    for copy in hops.values():
+        copy.wait_send()
+
+
+def collect_kernel(weight_ref, part_ref, out_ref, recvz, send1, recv1, send2, recv2, semz, sem1, sem2):
+    n, m = lax.axis_size("dp"), lax.axis_size("tensor")
+    me, t = lax.axis_index("dp"), lax.axis_index("tensor")
+    f32 = jnp.float32
+
+    barrier = pltpu.get_barrier_semaphore()
+    for k in range(1, n):
+        pl.semaphore_signal(
+            barrier, inc=1, device_id=(lax.rem(me + k, n), t), device_id_type=MESH
+        )
+    for k in range(1, m):
+        pl.semaphore_signal(
+            barrier, inc=1, device_id=(me, lax.rem(t + k, m)), device_id_type=MESH
+        )
+    pl.semaphore_wait(barrier, n + m - 2)
+
+    copies = []
+    for k in range(1, m):
+        peer = lax.rem(t + k, m)
+        copy = pltpu.make_async_remote_copy(
+            src_ref=part_ref.at[peer],
+            dst_ref=recvz.at[k],
+            send_sem=semz.at[0, k],
+            recv_sem=semz.at[1, k],
+            device_id=(me, peer),
+            device_id_type=MESH,
+        )
+        copy.start()
+        copies.append(copy)
+    for copy in copies:
+        copy.wait_recv()
+    firsts = []
+    for k in range(n):
+        chunk = lax.rem(me + k, n)
+        total = part_ref[t, chunk].astype(f32)
+        for z in range(1, m):
+            total = total + recvz[z, chunk].astype(f32)
+        if k == 0:
+            recv1[me] = total.astype(recv1.dtype)
+            continue
+        send1[k] = total.astype(send1.dtype)
+        copy = pltpu.make_async_remote_copy(
+            src_ref=send1.at[k],
+            dst_ref=recv1.at[me],
+            send_sem=sem1.at[0, k],
+            recv_sem=sem1.at[1, k],
+            device_id=(chunk, t),
+            device_id_type=MESH,
+        )
+        copy.start()
+        firsts.append(copy)
+    for copy in firsts:
+        copy.wait_recv()
+    seconds = []
+    for k in range(n):
+        peer = lax.rem(me + k, n)
+        total = weight_ref[peer, 0] * recv1[0].astype(f32)
+        for s in range(1, n):
+            total = total + weight_ref[peer, s] * recv1[s].astype(f32)
+        if k == 0:
+            recv2[me] = total.astype(recv2.dtype)
+            continue
+        send2[k] = total.astype(send2.dtype)
+        copy = pltpu.make_async_remote_copy(
+            src_ref=send2.at[k],
+            dst_ref=recv2.at[me],
+            send_sem=sem2.at[0, k],
+            recv_sem=sem2.at[1, k],
+            device_id=(peer, t),
+            device_id_type=MESH,
+        )
+        copy.start()
+        seconds.append(copy)
+    for copy in seconds:
+        copy.wait_recv()
+    for chunk in range(n):
+        out_ref[chunk] = recv2[chunk].astype(out_ref.dtype)
+    for copy in copies + firsts + seconds:
+        copy.wait_send()
+
+
+def dot_nn(a, b):
+    return jnp.dot(a, b, preferred_element_type=jnp.float32)
+
+
+def dot_nt(a, b):
+    return lax.dot_general(a, b, (((1,), (1,)), ((), ())), preferred_element_type=jnp.float32)
+
+
+def dot_tn(a, b):
+    return lax.dot_general(a, b, (((0,), (0,)), ((), ())), preferred_element_type=jnp.float32)
+
+
+def compute_kernel(
+    n, limit_ref, x_ref, gain_ref, cos_ref, sin_ref, posr_ref, posc_ref,
+    wq_ref, wk_ref, wv_ref, cot_ref, out_ref, grad_ref, normed, acc, inv_ref,
+):
+    step = pl.program_id(0)
+    m, rows, width = x_ref.shape
+    model_width = m * width
+    f32, bf16 = jnp.float32, jnp.bfloat16
+    chunk = rows // n
+    lead = chunk // 3
+    limit = limit_ref[0]
+
+    def prompt_rows(value):
+        return value.reshape(n, chunk, value.shape[-1])[:, chunk - lead :].reshape(
+            n * lead, value.shape[-1]
+        )
+
+    @pl.when(step == 0)
+    def _():
+        square = jnp.zeros((rows, 1), f32)
+        for z in range(m):
+            wide = x_ref[z].astype(f32)
+            square = square + jnp.sum(wide * wide, axis=1, keepdims=True)
+        inv = lax.rsqrt(square * (1.0 / model_width) + 1e-05)
+        inv_ref[...] = jnp.broadcast_to(inv, inv_ref.shape)
+        for z in range(m):
+            normed[z] = (x_ref[z].astype(f32) * inv * gain_ref[z]).astype(bf16)
+
+    def project(w_ref):
+        total = dot_nn(normed[0], w_ref[:width])
+        for z in range(1, m):
+            total = total + dot_nn(normed[z], w_ref[z * width : (z + 1) * width])
+        return total
+
+    cosine, sine = cos_ref[...], sin_ref[...]
+    cosine_p, sine_p = prompt_rows(cosine), prompt_rows(sine)
+    row_pos, col_pos = posr_ref[...], posc_ref[...]
+    allowed = (col_pos <= row_pos) & (col_pos < limit)
+    live = row_pos < limit
+    scale = 1.0 / math.sqrt(HD)
+    q_all, k_all, v_all = project(wq_ref), project(wk_ref), project(wv_ref)
+    grads_q, grads_k, grads_v = [], [], []
+    for h in range(wq_ref.shape[1] // HD):
+        at = slice(h * HD, (h + 1) * HD)
+        q, k, v = q_all[:, at], k_all[:, at], v_all[:, at].astype(bf16)
+        q = (q * cosine + pltpu.roll(q, HD // 2, 1) * sine).astype(bf16)
+        k = (k * cosine + pltpu.roll(k, HD // 2, 1) * sine).astype(bf16)
+        scores = jnp.where(allowed, dot_nt(q, k) * scale, -1e30)
+        peak = jnp.max(scores, axis=1, keepdims=True)
+        weights = jnp.where(allowed, jnp.exp(scores - peak), 0.0)
+        probs = weights / jnp.sum(weights, axis=1, keepdims=True)
+        low = probs.astype(bf16)
+        out_ref[:, at] = jnp.where(live, dot_nn(low, v), 0.0).astype(bf16)
+        upstream = jnp.where(live, cot_ref[:, at].astype(f32), 0.0).astype(bf16)
+        grad_prob = dot_nt(upstream, v)
+        delta = jnp.sum(probs * grad_prob, axis=1, keepdims=True)
+        grad_score = probs * (grad_prob - delta)
+        low_score = grad_score.astype(bf16)
+        gq = dot_nn(prompt_rows(grad_score).astype(bf16), k) * scale
+        gk = prompt_rows(dot_tn(low_score, q)) * scale
+        gv = prompt_rows(dot_tn(low, upstream))
+        gq = gq * cosine_p - pltpu.roll(gq, HD // 2, 1) * sine_p
+        gk = gk * cosine_p - pltpu.roll(gk, HD // 2, 1) * sine_p
+        grads_q.append(gq.astype(bf16))
+        grads_k.append(gk.astype(bf16))
+        grads_v.append(gv.astype(bf16))
+    grads_q = jnp.concatenate(grads_q, axis=1)
+    grads_k = jnp.concatenate(grads_k, axis=1)
+    grads_v = jnp.concatenate(grads_v, axis=1)
+    first = step == 0
+    for z in range(m):
+        at = slice(z * width, (z + 1) * width)
+        total = (
+            dot_nt(grads_q, wq_ref[at])
+            + dot_nt(grads_k, wk_ref[at])
+            + dot_nt(grads_v, wv_ref[at])
+        )
+        acc[z] = jnp.where(first, total, acc[z] + total)
+
+    @pl.when(step == pl.num_programs(0) - 1)
+    def _():
+        inv = prompt_rows(inv_ref[...])[:, :1]
+        dots = jnp.zeros((n * lead, 1), f32)
+        for z in range(m):
+            scaled = acc[z] * gain_ref[z]
+            acc[z] = scaled
+            wide = prompt_rows(x_ref[z].astype(f32))
+            dots = dots + jnp.sum(scaled * wide, axis=1, keepdims=True)
+        factor = inv * inv * inv * (dots * (1.0 / model_width))
+        for z in range(m):
+            wide = prompt_rows(x_ref[z].astype(f32))
+            grad_ref[z] = (inv * acc[z] - wide * factor).astype(bf16)
+
+
+def fast_device(text, prompts, gain, w_query, w_key, w_value, cotangent, task_of, lengths, slot):
+    n, m = lax.axis_size("dp"), lax.axis_size("tensor")
+    f32, bf16 = jnp.float32, jnp.bfloat16
+    me = lax.axis_index("dp")
+    seq, width = text.shape[1], text.shape[2]
+    p_len = prompts.shape[1]
+    ct = seq // n
+    cp = ct // 2
+    chunk = ct + cp
+    rows = n * chunk
+    heads = w_query.shape[1]
+    places = jnp.arange(n, dtype=jnp.int32)
+    matching = slot[None, :] == places[:, None]
+    source_slot = jnp.sum(jnp.where(matching, places[None, :], 0), axis=1)
+    task_slot = jnp.sum(jnp.where(matching, task_of[None, :], 0), axis=1)
+    length_slot = jnp.sum(jnp.where(matching, lengths[None, :], 0), axis=1)
+    limit = p_len + lax.dynamic_slice_in_dim(length_slot, me, 1)
+    weight = (places[:, None] == task_slot[None, :]).astype(f32)
+
+    def interleave(tail, lead):
+        lead = jnp.pad(lead, ((0, n * cp - p_len), (0, 0)))
+        parts = [tail.reshape(n, ct, -1), lead.reshape(n, cp, -1)]
+        return jnp.concatenate(parts, axis=1)
+
+    smem = pl.BlockSpec(memory_space=pltpu.SMEM)
+    vmem = pl.BlockSpec(memory_space=pltpu.VMEM)
+    chunks = interleave(text[0], prompts[0])
+    gathered = pl.pallas_call(
+        dispatch_kernel,
+        out_shape=jax.ShapeDtypeStruct((m, n, chunk, width), bf16),
+        in_specs=[smem, smem, vmem],
+        out_specs=vmem,
+        scratch_shapes=[
+            pltpu.VMEM((n, chunk, width), bf16),
+            pltpu.VMEM((n, chunk, width), bf16),
+            pltpu.SemaphoreType.DMA((2, n)),
+            pltpu.SemaphoreType.DMA((2, n)),
+            pltpu.SemaphoreType.DMA((2, 2, m // 2 + 1, n)),
+        ],
+        compiler_params=pltpu.CompilerParams(collective_id=0, has_side_effects=True),
+    )(source_slot, task_slot, chunks)
+    x = gathered.reshape(m, rows, width)
+
+    row = jnp.arange(rows, dtype=jnp.int32)
+    j, i = row // chunk, row % chunk
+    lead_pos = j * cp + i - ct
+    lead_pos = jnp.where(lead_pos < p_len, lead_pos, PAD_POS)
+    pos = jnp.where(i < ct, p_len + j * ct + i, lead_pos)
+    half = HD // 2
+    frequency = 10000.0 ** (-jnp.arange(half, dtype=f32) / half)
+    angle = jnp.where(pos < PAD_POS, pos, 0).astype(f32)[:, None] * frequency[None, :]
+    cosine = jnp.concatenate([jnp.cos(angle)] * 2, axis=1)
+    sine = jnp.concatenate([-jnp.sin(angle), jnp.sin(angle)], axis=1)
+    cot = interleave(cotangent[0, p_len:], cotangent[0, :p_len]).reshape(rows, heads)
+    group = 2 * HD if heads % (2 * HD) == 0 else HD
+
+    def whole(*shape):
+        return pl.BlockSpec(shape, lambda g: (0,) * len(shape))
+
+    w_spec = pl.BlockSpec((m * width, group), lambda g: (0, g))
+    r_spec = pl.BlockSpec((rows, group), lambda g: (0, g))
+    out, part = pl.pallas_call(
+        functools.partial(compute_kernel, n),
+        grid=(heads // group,),
+        out_shape=(
+            jax.ShapeDtypeStruct((rows, heads), bf16),
+            jax.ShapeDtypeStruct((m, n * cp, width), bf16),
+        ),
+        in_specs=[
+            smem,
+            whole(m, rows, width),
+            whole(m, 1, width),
+            whole(rows, HD),
+            whole(rows, HD),
+            whole(rows, 1),
+            whole(1, rows),
+            w_spec,
+            w_spec,
+            w_spec,
+            r_spec,
+        ],
+        out_specs=(r_spec, whole(m, n * cp, width)),
+        scratch_shapes=[
+            pltpu.VMEM((m, rows, width), bf16),
+            pltpu.VMEM((m, n * cp, width), f32),
+            pltpu.VMEM((rows, HD), f32),
+        ],
+        compiler_params=pltpu.CompilerParams(vmem_limit_bytes=60 * 2**20),
+    )(
+        limit, x, gain.reshape(m, 1, width), cosine, sine, pos[:, None], pos[None, :],
+        w_query, w_key, w_value, cot,
+    )
+    collected = pl.pallas_call(
+        collect_kernel,
+        out_shape=jax.ShapeDtypeStruct((n, cp, width), f32),
+        in_specs=[smem, vmem],
+        out_specs=vmem,
+        scratch_shapes=[
+            pltpu.VMEM((m, n, cp, width), bf16),
+            pltpu.VMEM((n, cp, width), bf16),
+            pltpu.VMEM((n, cp, width), bf16),
+            pltpu.VMEM((n, cp, width), bf16),
+            pltpu.VMEM((n, cp, width), bf16),
+            pltpu.SemaphoreType.DMA((2, m)),
+            pltpu.SemaphoreType.DMA((2, n)),
+            pltpu.SemaphoreType.DMA((2, n)),
+        ],
+        compiler_params=pltpu.CompilerParams(collective_id=1, has_side_effects=True),
+    )(weight, part.reshape(m, n, cp, width))
+    prompt_grad = collected.reshape(n * cp, width)[:p_len][None]
+    out = out.reshape(n, chunk, heads)
+    lead = out[:, ct:].reshape(n * cp, heads)[:p_len]
+    attn_out = jnp.concatenate([lead, out[:, :ct].reshape(seq, heads)], axis=0)[None]
+    return (attn_out, prompt_grad)
+
+
+def choose(text, prompts, *rest):
+    n, m = lax.axis_size("dp"), lax.axis_size("tensor")
+    seq, p_len = text.shape[1], prompts.shape[1]
+    fits = (
+        text.shape[0] == 1
+        and prompts.shape[0] == 1
+        and m >= 3
+        and n >= 2
+        and seq % (32 * n) == 0
+        and p_len <= seq // 2
+        and text.shape[2] % 128 == 0
+    )
+    return (fast_device if fits else on_device)(text, prompts, *rest)
+
+
 def solution(mesh):
     in_specs = (
         P("dp", None, "tensor"),
@@ -210,5 +625,5 @@
     )
     out_specs = (P("dp", None, "tensor"), P("dp", None, "tensor"))
     return jax.shard_map(
-        on_device, mesh=mesh, in_specs=in_specs, out_specs=out_specs, check_vma=False
-    )
+        choose, mesh=mesh, in_specs=in_specs, out_specs=out_specs, check_vma=False
+    )

time: 274 us -> 180 us (0.66); the launches traced: 270 us -> 180 us
  Pallas kernels: 0 us -> 164 us
  waiting for transfers between devices: 91.6 us -> 0 us
  local copies, waits for them, and re-layouts: 53 us -> 5.89 us
  matrix products: 37.9 us -> 0 us
  blocking collectives: 31 us -> 0 us
  other arithmetic: 26.2 us -> 7.91 us
  starting transfers between devices: 14.9 us -> 0 us
  between operations: 15.3 us -> 1.4 us
    pallas_call x0 -> x3, Pallas kernels: none -> 164 us  [the longest x1 83.2 us: fast_device(): pl.pallas_call(dispatch_kernel, out_shape=jax.ShapeDtypeStruct((m, n, chu...]
    unnamed x71 -> x6, local copies, waits for them, and re-layouts: 46.4 us -> 0.01 us
    reduce_scatter x1 -> x0, waiting for transfers between devices: 44.3 us -> none  [on_device(): lax.psum_scatter(grad_part, 'tensor', scatter_dimension=2, tiled=True)]
    all_gather x1 -> x0, waiting for transfers between devices: 35 us -> none  [on_device(): full_rows = lax.all_gather(local_rows, 'tensor', axis=2, tiled=True)]
    dot_general x14 -> x0, matrix products: 34.2 us -> none  [the longest x3 16.8 us: project(): jnp.dot(normed, matrix, preferred_element_type=jnp.float32)]
    all_to_all x2 -> x0, blocking collectives: 31 us -> none  [the longest x1 16.9 us: on_device(): lax.all_to_all(placed, 'dp', split_axis=0, concat_axis=3, tiled=True)[0]]
    all_to_all x3 -> x0, starting transfers between devices: 14.6 us -> none  [the longest x1 5.9 us: on_device(): lax.all_to_all(per_task, 'dp', split_axis=0, concat_axis=2, tiled=True)]
    unnamed x6 -> x0, other arithmetic: 14.3 us -> none
  transfers between devices with their start and end apart: 5 -> 0, of which waited for: 4 -> 0; matrix products, arithmetic and copies ran while one was open for 19% -> 0% of each run, Pallas kernels for 0% -> 0%
where the time goes in v1:
time: 180 us
  Pallas kernels  164 us (91%)
  other arithmetic  7.91 us (4%)
  local copies, waits for them, and re-layouts  5.89 us (3%)
    pallas_call x1, Pallas kernels, fast_device(): pl.pallas_call(dispatch_kernel, out_shape=jax.ShapeDtypeStruct((m, n, chu...  83.2 us
    pallas_call x1, Pallas kernels, fast_device(): pl.pallas_call(collect_kernel, out_shape=jax.ShapeDtypeStruct((n, cp, wid...  46.7 us
    pallas_call x1, Pallas kernels, fast_device(): pl.pallas_call(functools.partial(compute_kernel, n), grid=(heads // group...  34.6 us

profile of v1, /device:TPU:11, one launch (start us, length us, event | category | flops | bytes accessed | tf_op | source)
XLA Modules:
  0.0 179.6 jit_solution(10056479657467083050)
XLA Ops:
  0.6 0.0 copy-start
  0.6 1.4 select_reduce_fusion
  2.1 0.6 dynamic_slice.3
  3.3 0.8 fusion.12
  4.1 0.9 pad_maximum_fusion.2
  5.0 1.0 pad.8
  6.0 0.0 copy-done
  6.0 1.0 pad_maximum_fusion.inp_ref
  7.0 0.0 copy-start.1
  7.0 83.2 %shard_map.113 = bf16[4,8,48,1280]{3,2,1,0:T(8,128)(2,1)} custom-call(s32[8]{0:T(128)} %get-tuple-element.7.source_ref, s32[8]{0:T(128)} %get-tuple-element.6.task_ref, bf16[8,48,1280]{2,1,0:T(8,128)(2,1)} %pad_maximum_fusion.inp_ref), custom_call_target="tpu_custom_call" | custom-call | tf_op jit(solution)/shard_map/pallas_call | solution.py:509
  90.2 0.0 copy-done.1
  90.2 0.1 slice.18
  90.4 0.9 pad_maximum_fusion.1
  91.2 0.8 fusion.9.posr_ref
  92.0 0.6 compare_select_fusion.2.posc_ref
  92.6 34.6 %shard_map.114 = (bf16[384,768]{1,0:T(8,128)(2,1)}, bf16[4,128,1280]{2,1,0:T(8,128)(2,1)}) custom-call(s32[1]{0:T(128)S(6)} %add.170.limit_ref, bf16[4,384,1280]{2,1,0:T(8,128)(2,1)} %bitcast.17, f32[4,1,1280]{2,1,0:T(1,128)} %bitcast.30, f32[384,128]{1,0:T(8,128)} %get-tuple-element.12.cos_ref, f32[384,128]{1,0:T(8,128)} %get-tuple-element.13.sin_ref, ...), custom_call_target="tpu_custom_call" | custom-call | tf_op jit(solution)/shard_map/pallas_call | solution.py:543
  127.2 0.0 copy-start.2
  127.2 1.0 slice.26
  128.2 0.9 slice.24
  129.2 0.9 maximum_bitcast_fusion
  130.1 0.0 copy-done.2
  130.1 0.6 fusion.17.weight_ref
  130.7 46.7 %shard_map.115 = f32[8,16,1280]{2,1,0:T(8,128)} custom-call(f32[8,8]{1,0:T(8,128)} %fusion.17.weight_ref, bf16[4,8,16,1280]{3,2,1,0:T(8,128)(2,1)} %bitcast.22), custom_call_target="tpu_custom_call" | custom-call | tf_op jit(solution)/shard_map/pallas_call | solution.py:574
  177.4 1.1 slice.27
  178.5 1.1 broadcast_in_dim.58
  (5 shorter events, 0.1 us)
Async XLA Ops:
  0.6 5.4 %copy-start = (bf16[1,256,1280]{2,1,0:T(8,128)(2,1)S(1)}, bf16[1,256,1280]{2,1,0:T(8,128)(2,1)}, u32[]{:S(2)}) copy-start(bf16[1,256,1280]{2,1,0:T(8,128)(2,1)} %param.10) | copy-start | bytes 1966084
  7.0 83.2 %copy-start.1 = (bf16[1,356,768]{2,1,0:T(8,128)(2,1)S(1)}, bf16[1,356,768]{2,1,0:T(8,128)(2,1)}, u32[]{:S(2)}) copy-start(bf16[1,356,768]{2,1,0:T(8,128)(2,1)} %param.16) | copy-start | bytes 1640452
  127.2 2.9 %copy-start.2 = (s32[8]{0:T(128)S(1)}, s32[8]{0:T(128)}, u32[]{:S(2)}) copy-start(s32[8]{0:T(128)} %get-tuple-element.6.task_ref) | copy-start | bytes 100

commit v2 on v0

--- a/solution.py
+++ b/solution.py
@@ -1,8 +1,11 @@
+import functools
 import math
 
 import jax
 import jax.numpy as jnp
 from jax import lax
+from jax.experimental import pallas as pl
+from jax.experimental.pallas import tpu as pltpu
 from jax.sharding import PartitionSpec as P
 
 HD = 128
@@ -195,6 +198,375 @@
     return (output, prompt_grad)
 
 
+MESH = pl.DeviceIdType.MESH
+PAD_POS = 1 << 20
+
+
+def dot_nn(a, b):
+    return jnp.dot(a, b, preferred_element_type=jnp.float32)
+
+
+def dot_nt(a, b):
+    return lax.dot_general(a, b, (((1,), (1,)), ((), ())), preferred_element_type=jnp.float32)
+
+
+def dot_tn(a, b):
+    return lax.dot_general(a, b, (((0,), (0,)), ((), ())), preferred_element_type=jnp.float32)
+
+
+def step_kernel(
+    p_len, slot_ref, task_ref, length_ref, inp_ref, gain_ref, cos_ref, sin_ref, posr_ref, posc_ref,
+    cot_ref, wq_hbm, wk_hbm, wv_hbm, out_ref, grad_ref,
+    w_ref, recv, send, full, squares, qkv, grads, inv_ref, acc, part, recvz, send1, recv1, send2, recv2,
+    semw, sem1, sem2, semz, semq, semg, sem3, sem4,
+):
+    n, m = lax.axis_size("dp"), lax.axis_size("tensor")
+    me, t = lax.axis_index("dp"), lax.axis_index("tensor")
+    f32, bf16 = jnp.float32, jnp.bfloat16
+    right, left = lax.rem(t + 1, m), lax.rem(t + m - 1, m)
+    _, chunk, width = inp_ref.shape
+    blocks, model_width, group = w_ref.shape
+    per = blocks // 3
+    rows = n * chunk
+    lead = chunk // 3
+    split = chunk - lead
+
+    def pick(place, values):
+        total = jnp.int32(0)
+        for e in range(n):
+            total = jnp.maximum(total, jnp.where(slot_ref[e] == place, values(e), 0))
+        return total
+
+    def source_of(place):
+        return pick(place, lambda e: e)
+
+    def task_at(place):
+        return pick(place, lambda e: task_ref[e])
+
+    def remote(src, dst, sems, device):
+        copy = pltpu.make_async_remote_copy(
+            src_ref=src,
+            dst_ref=dst,
+            send_sem=sems[0],
+            recv_sem=sems[1],
+            device_id=device,
+            device_id_type=MESH,
+        )
+        copy.start()
+        return copy
+
+    loads = []
+    for i, hbm in enumerate((wq_hbm, wk_hbm, wv_hbm)):
+        for g in range(per):
+            at = i * per + g
+            load = pltpu.make_async_copy(
+                hbm.at[:, g * group : (g + 1) * group], w_ref.at[at], semw.at[at]
+            )
+            load.start()
+            loads.append(load)
+
+    barrier = pltpu.get_barrier_semaphore()
+    for k in range(1, n):
+        pl.semaphore_signal(
+            barrier, inc=1, device_id=(lax.rem(me + k, n), t), device_id_type=MESH
+        )
+    for k in range(1, m):
+        pl.semaphore_signal(
+            barrier, inc=1, device_id=(me, lax.rem(t + k, m)), device_id_type=MESH
+        )
+    pl.semaphore_wait(barrier, n + m - 2)
+
+    first = []
+    for k in range(1, n):
+        peer = lax.rem(me + k, n)
+        sems = (sem1.at[0, k], sem1.at[1, k])
+        first.append(remote(inp_ref.at[peer], recv.at[me], sems, (peer, t)))
+    recv[me] = inp_ref[me]
+    for copy in first:
+        copy.wait_recv()
+
+    second = []
+    for k in range(1, n):
+        peer = lax.rem(me + k, n)
+        send[k, :split] = recv[source_of(peer), :split]
+        send[k, split:] = recv[task_at(peer), split:]
+        sems = (sem2.at[0, k], sem2.at[1, k])
+        second.append(remote(send.at[k], full.at[t, me], sems, (peer, t)))
+    full[t, me, :split] = recv[source_of(me), :split]
+    full[t, me, split:] = recv[task_at(me), split:]
+
+    def hop(origin, k, distance, way):
+        place = full.at[origin, lax.rem(me + n - k, n)]
+        sems = (semz.at[0, way, distance, k], semz.at[1, way, distance, k])
+        return remote(place, place, sems, (me, left if way else right))
+
+    def reach(k, way):
+        half = m // 2
+        return half if way == k % 2 else m - 1 - half
+
+    hops = {}
+    for k in range(n):
+        if k:
+            second[k - 1].wait_recv()
+        for way in (0, 1):
+            hops[way, 1, k] = hop(t, k, 1, way)
+
+    own = full[t].reshape(rows, width).astype(f32)
+    square = jnp.sum(own * own, axis=1, keepdims=True)
+    squares[0] = jnp.broadcast_to(square, (rows, 128)).T[:8]
+    shared = []
+    for k in range(1, m):
+        peer = lax.rem(t + k, m)
+        sems = (semq.at[0, k], semq.at[1, k])
+        shared.append(remote(squares.at[0], squares.at[k], sems, (me, peer)))
+
+    def origin_of(distance, way):
+        return lax.rem(t + (m - distance if way == 0 else distance), m)
+
+    def receive(distance):
+        for k in range(n):
+            for way in (0, 1):
+                if distance <= reach(k, way):
+                    hops[way, distance, k].wait_recv()
+                    if distance < reach(k, way):
+                        origin = origin_of(distance, way)
+                        hops[way, distance + 1, k] = hop(origin, k, distance + 1, way)
+
+    def project(origin, fresh):
+        wide = full[origin].reshape(rows, width).astype(f32)
+        normed = (wide * inv_ref[:, :1] * gain_ref[origin]).astype(bf16)
+        deep = pl.ds(pl.multiple_of(origin * width, width), width)
+
+        def body(b, carry):
+            product = dot_nn(normed, w_ref[b, deep, :])
+            qkv[b] = product if fresh else qkv[b] + product
+            return carry
+
+        lax.fori_loop(0, blocks, body, 0)
+
+    receive(1)
+    for copy in shared:
+        copy.wait_recv()
+    square = squares[0]
+    for k in range(1, m):
+        square = square + squares[k]
+    square = jnp.broadcast_to(square[:1], (128, rows)).T
+    inv_ref[...] = lax.rsqrt(square * (1.0 / model_width) + 1e-05)
+    for load in loads:
+        load.wait()
+    project(t, True)
+    project(origin_of(1, 0), False)
+    project(origin_of(1, 1), False)
+    for distance in range(2, m // 2 + 1):
+        receive(distance)
+        project(origin_of(distance, 0), False)
+        if 2 * distance != m:
+            project(origin_of(distance, 1), False)
+
+    def prompt_rows(value):
+        return value.reshape(n, chunk, value.shape[-1])[:, split:].reshape(
+            n * lead, value.shape[-1]
+        )
+
+    limit = p_len + pick(me, lambda e: length_ref[e])
+    scale = 1.0 / math.sqrt(HD)
+
+    def heads(g, carry):
+        cosine, sine = cos_ref[...], sin_ref[...]
+        cosine_p, sine_p = prompt_rows(cosine), prompt_rows(sine)
+        row_pos, col_pos = posr_ref[...], posc_ref[...]
+        allowed = (col_pos <= row_pos) & (col_pos < limit)
+        live = row_pos < limit
+        for h in range(group // HD):
+            at = slice(h * HD, (h + 1) * HD)
+            far = pl.ds(pl.multiple_of(g * group + h * HD, HD), HD)
+            q, k = qkv[g, :, at], qkv[per + g, :, at]
+            v = qkv[2 * per + g, :, at].astype(bf16)
+            q = (q * cosine + pltpu.roll(q, HD // 2, 1) * sine).astype(bf16)
+            k = (k * cosine + pltpu.roll(k, HD // 2, 1) * sine).astype(bf16)
+            scores = jnp.where(allowed, dot_nt(q, k) * scale, -1e30)
+            peak = jnp.max(scores, axis=1, keepdims=True)
+            weights = jnp.where(allowed, jnp.exp(scores - peak), 0.0)
+            probs = weights / jnp.sum(weights, axis=1, keepdims=True)
+            low = probs.astype(bf16)
+            out_ref[:, far] = jnp.where(live, dot_nn(low, v), 0.0).astype(bf16)
+            upstream = jnp.where(live, cot_ref[:, far].astype(f32), 0.0).astype(bf16)
+            grad_prob = dot_nt(upstream, v)
+            delta = jnp.sum(probs * grad_prob, axis=1, keepdims=True)
+            grad_score = probs * (grad_prob - delta)
+            gq = dot_nn(prompt_rows(grad_score).astype(bf16), k) * scale
+            gk = prompt_rows(dot_tn(grad_score.astype(bf16), q)) * scale
+            gv = prompt_rows(dot_tn(low, upstream))
+            gq = gq * cosine_p - pltpu.roll(gq, HD // 2, 1) * sine_p
+            gk = gk * cosine_p - pltpu.roll(gk, HD // 2, 1) * sine_p
+            grads[g, :, at] = gq.astype(bf16)
+            grads[per + g, :, at] = gk.astype(bf16)
+            grads[2 * per + g, :, at] = gv.astype(bf16)
+        return carry
+
+    lax.fori_loop(0, per, heads, 0)
+
+    def prompts_of(z):
+        return full[z, :, split:, :].astype(f32).reshape(n * lead, width)
+
+    def back(z, dots):
+        deep = pl.ds(pl.multiple_of(z * width, width), width)
+        total = dot_nt(grads[0], w_ref[0, deep, :])
+        for b in range(1, blocks):
+            total = total + dot_nt(grads[b], w_ref[b, deep, :])
+        total = total * gain_ref[z]
+        acc[z] = total
+        return dots + jnp.sum(total * prompts_of(z), axis=1, keepdims=True)
+
+    dots = lax.fori_loop(0, m, back, jnp.zeros((n * lead, 1), f32))
+    inv = prompt_rows(inv_ref[...])[:, :1]
+    factor = inv * inv * inv * (dots * (1.0 / model_width))
+
+    partial = {}
+    for step in range(m):
+        z = lax.rem(t + (2, 1, 3, 0)[step] if m == 4 else t + m - 1 - step, m)
+        value = (inv * acc[z] - prompts_of(z) * factor).astype(bf16)
+        part[z] = value.reshape(n, lead, width)
+        if step < m - 1:
+            for k in range(n):
+                at = lax.rem(me + k, n)
+                sems = (semg.at[0, step, k], semg.at[1, step, k])
+                partial[step, k] = remote(part.at[z, at], recvz.at[step, at], sems, (me, z))
+
+    third = []
+    for k in range(n):
+        at = lax.rem(me + k, n)
+        total = part[t, at].astype(f32)
+        for step in range(m - 1):
+            partial[step, k].wait_recv()
+            total = total + recvz[step, at].astype(f32)
+        if k == 0:
+            recv1[me] = total.astype(bf16)
+            continue
+        send1[k] = total.astype(bf16)
+        sems = (sem3.at[0, k], sem3.at[1, k])
+        third.append(remote(send1.at[k], recv1.at[me], sems, (at, t)))
+    for copy in third:
+        copy.wait_recv()
+    tasks = [task_at(s) for s in range(n)]
+    fourth = []
+    for k in range(n):
+        peer = lax.rem(me + k, n)
+        total = jnp.zeros((lead, width), f32)
+        for s in range(n):
+            hit = jnp.where(tasks[s] == peer, 1.0, 0.0)
+            total = total + hit * recv1[s].astype(f32)
+        if k == 0:
+            recv2[me] = total.astype(bf16)
+            continue
+        send2[k] = total.astype(bf16)
+        sems = (sem4.at[0, k], sem4.at[1, k])
+        fourth.append(remote(send2.at[k], recv2.at[me], sems, (peer, t)))
+    for copy in fourth:
+        copy.wait_recv()
+    for at in range(n):
+        grad_ref[at] = recv2[at].astype(f32)
+    for copy in first + second + list(hops.values()) + shared:
+        copy.wait_send()
+    for copy in list(partial.values()) + third + fourth:
+        copy.wait_send()
+
+
+def fast_device(text, prompts, gain, w_query, w_key, w_value, cotangent, task_of, lengths, slot):
+    n, m = lax.axis_size("dp"), lax.axis_size("tensor")
+    f32, bf16 = jnp.float32, jnp.bfloat16
+    seq, width = text.shape[1], text.shape[2]
+    p_len = prompts.shape[1]
+    ct = seq // n
+    cp = ct // 2
+    chunk = ct + cp
+    rows = n * chunk
+    heads = w_query.shape[1]
+
+    def interleave(tail, lead):
+        lead = jnp.pad(lead, ((0, n * cp - p_len), (0, 0)))
+        parts = [tail.reshape(n, ct, -1), lead.reshape(n, cp, -1)]
+        return jnp.concatenate(parts, axis=1)
+
+    row = jnp.arange(rows, dtype=jnp.int32)
+    j, i = row // chunk, row % chunk
+    lead_pos = j * cp + i - ct
+    lead_pos = jnp.where(lead_pos < p_len, lead_pos, PAD_POS)
+    pos = jnp.where(i < ct, p_len + j * ct + i, lead_pos)
+    half = HD // 2
+    frequency = 10000.0 ** (-jnp.arange(half, dtype=f32) / half)
+    angle = jnp.where(pos < PAD_POS, pos, 0).astype(f32)[:, None] * frequency[None, :]
+    cosine = jnp.concatenate([jnp.cos(angle)] * 2, axis=1)
+    sine = jnp.concatenate([-jnp.sin(angle), jnp.sin(angle)], axis=1)
+    cot = interleave(cotangent[0, p_len:], cotangent[0, :p_len]).reshape(rows, heads)
+    group = 2 * HD if heads % (2 * HD) == 0 else HD
+    blocks = 3 * (heads // group)
+    smem = pl.BlockSpec(memory_space=pltpu.SMEM)
+    vmem = pl.BlockSpec(memory_space=pltpu.VMEM)
+    hbm = pl.BlockSpec(memory_space=pl.ANY)
+    dma = pltpu.SemaphoreType.DMA
+    out, collected = pl.pallas_call(
+        functools.partial(step_kernel, p_len),
+        out_shape=(
+            jax.ShapeDtypeStruct((rows, heads), bf16),
+            jax.ShapeDtypeStruct((n, cp, width), f32),
+        ),
+        in_specs=[smem] * 3 + [vmem] * 7 + [hbm] * 3,
+        out_specs=(vmem, vmem),
+        scratch_shapes=[
+            pltpu.VMEM((blocks, m * width, group), bf16),
+            pltpu.VMEM((n, chunk, width), bf16),
+            pltpu.VMEM((n, chunk, width), bf16),
+            pltpu.VMEM((m, n, chunk, width), bf16),
+            pltpu.VMEM((m, 8, rows), f32),
+            pltpu.VMEM((blocks, rows, group), f32),
+            pltpu.VMEM((blocks, n * cp, group), bf16),
+            pltpu.VMEM((rows, 128), f32),
+            pltpu.VMEM((m, n * cp, width), f32),
+            pltpu.VMEM((m, n, cp, width), bf16),
+            pltpu.VMEM((m - 1, n, cp, width), bf16),
+            pltpu.VMEM((n, cp, width), bf16),
+            pltpu.VMEM((n, cp, width), bf16),
+            pltpu.VMEM((n, cp, width), bf16),
+            pltpu.VMEM((n, cp, width), bf16),
+            dma((blocks,)),
+            dma((2, n)),
+            dma((2, n)),
+            dma((2, 2, m // 2 + 1, n)),
+            dma((2, m)),
+            dma((2, m, n)),
+            dma((2, n)),
+            dma((2, n)),
+        ],
+        compiler_params=pltpu.CompilerParams(
+            collective_id=0, has_side_effects=True, vmem_limit_bytes=63 * 2**20
+        ),
+    )(
+        slot, task_of, lengths, interleave(text[0], prompts[0]), gain.reshape(m, 1, width),
+        cosine, sine, pos[:, None], pos[None, :], cot, w_query, w_key, w_value,
+    )
+    prompt_grad = collected.reshape(n * cp, width)[:p_len][None]
+    out = out.reshape(n, chunk, heads)
+    lead = out[:, ct:].reshape(n * cp, heads)[:p_len]
+    attn_out = jnp.concatenate([lead, out[:, :ct].reshape(seq, heads)], axis=0)[None]
+    return (attn_out, prompt_grad)
+
+
+def choose(text, prompts, *rest):
+    n, m = lax.axis_size("dp"), lax.axis_size("tensor")
+    seq, p_len = text.shape[1], prompts.shape[1]
+    fits = (
+        text.shape[0] == 1
+        and prompts.shape[0] == 1
+        and m >= 3
+        and n >= 2
+        and seq % (32 * n) == 0
+        and p_len <= seq // 2
+        and text.shape[2] % 128 == 0
+    )
+    return (fast_device if fits else on_device)(text, prompts, *rest)
+
+
 def solution(mesh):
     in_specs = (
         P("dp", None, "tensor"),
@@ -210,5 +582,5 @@
     )
     out_specs = (P("dp", None, "tensor"), P("dp", None, "tensor"))
     return jax.shard_map(
-        on_device, mesh=mesh, in_specs=in_specs, out_specs=out_specs, check_vma=False
-    )
+        choose, mesh=mesh, in_specs=in_specs, out_specs=out_specs, check_vma=False
+    )

time: 274 us -> 157 us (0.57); the launches traced: 270 us -> 157 us
  Pallas kernels: 0 us -> 145 us
  waiting for transfers between devices: 91.6 us -> 0 us
  local copies, waits for them, and re-layouts: 53 us -> 5.42 us
  matrix products: 37.9 us -> 0 us
  blocking collectives: 31 us -> 0 us
  other arithmetic: 26.2 us -> 5.92 us
  starting transfers between devices: 14.9 us -> 0 us
  between operations: 15.3 us -> 0.7 us
    pallas_call x0 -> x1, Pallas kernels: none -> 145 us  [fast_device(): pl.pallas_call(functools.partial(step_kernel, p_len), out_shape=(jax.Shap...]
    unnamed x71 -> x4, local copies, waits for them, and re-layouts: 46.4 us -> 0.01 us
    reduce_scatter x1 -> x0, waiting for transfers between devices: 44.3 us -> none  [on_device(): lax.psum_scatter(grad_part, 'tensor', scatter_dimension=2, tiled=True)]
    all_gather x1 -> x0, waiting for transfers between devices: 35 us -> none  [on_device(): full_rows = lax.all_gather(local_rows, 'tensor', axis=2, tiled=True)]
    dot_general x14 -> x0, matrix products: 34.2 us -> none  [the longest x3 16.8 us: project(): jnp.dot(normed, matrix, preferred_element_type=jnp.float32)]
    all_to_all x2 -> x0, blocking collectives: 31 us -> none  [the longest x1 16.9 us: on_device(): lax.all_to_all(placed, 'dp', split_axis=0, concat_axis=3, tiled=True)[0]]
    all_to_all x3 -> x0, starting transfers between devices: 14.6 us -> none  [the longest x1 5.9 us: on_device(): lax.all_to_all(per_task, 'dp', split_axis=0, concat_axis=2, tiled=True)]
    unnamed x6 -> x0, other arithmetic: 14.3 us -> none
  transfers between devices with their start and end apart: 5 -> 0, of which waited for: 4 -> 0; matrix products, arithmetic and copies ran while one was open for 19% -> 0% of each run, Pallas kernels for 0% -> 0%
where the time goes in v2:
time: 157 us
  Pallas kernels  145 us (92%)
  other arithmetic  5.92 us (4%)
  local copies, waits for them, and re-layouts  5.42 us (3%)
    pallas_call x1, Pallas kernels, fast_device(): pl.pallas_call(functools.partial(step_kernel, p_len), out_shape=(jax.Shap...  145 us

profile of v2, /device:TPU:11, one launch (start us, length us, event | category | flops | bytes accessed | tf_op | source)
XLA Modules:
  0.0 156.6 jit_solution(1941006393161830307)
XLA Ops:
  0.6 0.6 compare_select_fusion.2.posc_ref
  1.3 0.9 slice_bitcast_fusion
  2.2 0.8 fusion.9.posr_ref
  3.0 0.0 copy-start
  3.0 1.0 pad.8
  4.1 1.1 slice.18
  5.2 0.9 pad_maximum_fusion.1
  6.0 0.8 fusion.12
  6.8 0.9 pad_maximum_fusion.2
  7.7 0.0 copy-done
  7.7 1.0 pad_maximum_fusion.inp_ref
  8.8 144.5 %shard_map.113 = (bf16[384,768]{1,0:T(8,128)(2,1)}, f32[8,16,1280]{2,1,0:T(8,128)}) custom-call(s32[8]{0:T(128)} %slot_ref.1, s32[8]{0:T(128)} %task_ref.1, s32[8]{0:T(128)} %length_ref.1, bf16[8,48,1280]{2,1,0:T(8,128)(2,1)} %pad_maximum_fusion.inp_ref, f32[4,1,1280]{2,1,0:T(1,128)} %bitcast.26, f32[384,128]{1,0:T(8,128)} %get-tuple-element.9.cos_ref, ...), custom_call_target="tpu_custom_call" | custom-call | tf_op jit(solution)/shard_map/pallas_call | solution.py:508
  153.3 0.0 copy-start.1
  153.3 1.1 slice.27
  154.5 1.1 broadcast_in_dim.23
  155.6 0.0 copy-done.1
  155.7 0.9 maximum_bitcast_fusion
  (6 shorter events, 0.1 us)
Async XLA Ops:
  3.0 4.7 %copy-start = (bf16[1,256,1280]{2,1,0:T(8,128)(2,1)S(1)}, bf16[1,256,1280]{2,1,0:T(8,128)(2,1)}, u32[]{:S(2)}) copy-start(bf16[1,256,1280]{2,1,0:T(8,128)(2,1)} %param.10) | copy-start | bytes 1966084
  153.3 2.3 %copy-start.1 = (bf16[384,768]{1,0:T(8,128)(2,1)S(1)}, bf16[384,768]{1,0:T(8,128)(2,1)}, u32[]{:S(2)}) copy-start(bf16[384,768]{1,0:T(8,128)(2,1)} %get-tuple-element.4) | copy-start | bytes 1769476

commit v3 on v2

--- a/solution.py
+++ b/solution.py
@@ -3,6 +3,7 @@
 
 import jax
 import jax.numpy as jnp
+import numpy as np
 from jax import lax
 from jax.experimental import pallas as pl
 from jax.experimental.pallas import tpu as pltpu
@@ -243,7 +244,7 @@
     def task_at(place):
         return pick(place, lambda e: task_ref[e])
 
-    def remote(src, dst, sems, device):
+    def remote(src, dst, sems, device, needed=None):
         copy = pltpu.make_async_remote_copy(
             src_ref=src,
             dst_ref=dst,
@@ -252,8 +253,14 @@
             device_id=device,
             device_id_type=MESH,
         )
-        copy.start()
+        if needed is None:
+            copy.start()
+        else:
+            pl.when(needed)(copy.start)
         return copy
+
+    def holds(at):
+        return at * lead < p_len
 
     loads = []
     for i, hbm in enumerate((wq_hbm, wk_hbm, wv_hbm)):
@@ -386,8 +393,8 @@
             k = (k * cosine + pltpu.roll(k, HD // 2, 1) * sine).astype(bf16)
             scores = jnp.where(allowed, dot_nt(q, k) * scale, -1e30)
             peak = jnp.max(scores, axis=1, keepdims=True)
-            weights = jnp.where(allowed, jnp.exp(scores - peak), 0.0)
-            probs = weights / jnp.sum(weights, axis=1, keepdims=True)
+            weights = jnp.exp(scores - peak)
+            probs = weights * (1.0 / jnp.sum(weights, axis=1, keepdims=True))
             low = probs.astype(bf16)
             out_ref[:, far] = jnp.where(live, dot_nn(low, v), 0.0).astype(bf16)
             upstream = jnp.where(live, cot_ref[:, far].astype(f32), 0.0).astype(bf16)
@@ -431,45 +438,67 @@
             for k in range(n):
                 at = lax.rem(me + k, n)
                 sems = (semg.at[0, step, k], semg.at[1, step, k])
-                partial[step, k] = remote(part.at[z, at], recvz.at[step, at], sems, (me, z))
+                partial[step, k] = remote(
+                    part.at[z, at], recvz.at[step, at], sems, (me, z), holds(at)
+                )
 
     third = []
     for k in range(n):
         at = lax.rem(me + k, n)
-        total = part[t, at].astype(f32)
-        for step in range(m - 1):
-            partial[step, k].wait_recv()
-            total = total + recvz[step, at].astype(f32)
-        if k == 0:
-            recv1[me] = total.astype(bf16)
-            continue
-        send1[k] = total.astype(bf16)
-        sems = (sem3.at[0, k], sem3.at[1, k])
-        third.append(remote(send1.at[k], recv1.at[me], sems, (at, t)))
-    for copy in third:
-        copy.wait_recv()
+
+        @pl.when(holds(at))
+        def _():
+            total = part[t, at].astype(f32)
+            for step in range(m - 1):
+                partial[step, k].wait_recv()
+                total = total + recvz[step, at].astype(f32)
+            if k == 0:
+                recv1[me] = total.astype(bf16)
+            else:
+                send1[k] = total.astype(bf16)
+
+        if k:
+            sems = (sem3.at[0, k], sem3.at[1, k])
+            third.append(remote(send1.at[k], recv1.at[me], sems, (at, t), holds(at)))
+
+    @pl.when(holds(me))
+    def _():
+        for copy in third:
+            copy.wait_recv()
+
     tasks = [task_at(s) for s in range(n)]
     fourth = []
     for k in range(n):
         peer = lax.rem(me + k, n)
-        total = jnp.zeros((lead, width), f32)
-        for s in range(n):
-            hit = jnp.where(tasks[s] == peer, 1.0, 0.0)
-            total = total + hit * recv1[s].astype(f32)
-        if k == 0:
-            recv2[me] = total.astype(bf16)
-            continue
-        send2[k] = total.astype(bf16)
-        sems = (sem4.at[0, k], sem4.at[1, k])
-        fourth.append(remote(send2.at[k], recv2.at[me], sems, (peer, t)))
-    for copy in fourth:
-        copy.wait_recv()
+
+        @pl.when(holds(me))
+        def _():
+            total = jnp.zeros((lead, width), f32)
+            for s in range(n):
+                hit = jnp.where(tasks[s] == peer, 1.0, 0.0)
+                total = total + hit * recv1[s].astype(f32)
+            if k == 0:
+                recv2[me] = total.astype(bf16)
+            else:
+                send2[k] = total.astype(bf16)
+
+        if k:
+            sems = (sem4.at[0, k], sem4.at[1, k])
+            fourth.append(remote(send2.at[k], recv2.at[me], sems, (peer, t), holds(me)))
+    for k in range(1, n):
+        pl.when(holds(lax.rem(me + n - k, n)))(fourth[k - 1].wait_recv)
     for at in range(n):
-        grad_ref[at] = recv2[at].astype(f32)
+        if at * lead < p_len:
+            grad_ref[at] = recv2[at].astype(f32)
+        else:
+            grad_ref[at] = jnp.zeros((lead, width), f32)
     for copy in first + second + list(hops.values()) + shared:
         copy.wait_send()
-    for copy in list(partial.values()) + third + fourth:
-        copy.wait_send()
+    for (_, k), copy in partial.items():
+        pl.when(holds(lax.rem(me + k, n)))(copy.wait_send)
+    for k in range(1, n):
+        pl.when(holds(lax.rem(me + k, n)))(third[k - 1].wait_send)
+        pl.when(holds(me))(fourth[k - 1].wait_send)
 
 
 def fast_device(text, prompts, gain, w_query, w_key, w_value, cotangent, task_of, lengths, slot):
@@ -488,14 +517,14 @@
         parts = [tail.reshape(n, ct, -1), lead.reshape(n, cp, -1)]
         return jnp.concatenate(parts, axis=1)
 
-    row = jnp.arange(rows, dtype=jnp.int32)
+    row = np.arange(rows, dtype=np.int32)
     j, i = row // chunk, row % chunk
     lead_pos = j * cp + i - ct
-    lead_pos = jnp.where(lead_pos < p_len, lead_pos, PAD_POS)
-    pos = jnp.where(i < ct, p_len + j * ct + i, lead_pos)
+    lead_pos = np.where(lead_pos < p_len, lead_pos, PAD_POS)
+    pos = np.where(i < ct, p_len + j * ct + i, lead_pos).astype(np.int32)
     half = HD // 2
     frequency = 10000.0 ** (-jnp.arange(half, dtype=f32) / half)
-    angle = jnp.where(pos < PAD_POS, pos, 0).astype(f32)[:, None] * frequency[None, :]
+    angle = jnp.asarray(np.where(pos < PAD_POS, pos, 0)).astype(f32)[:, None] * frequency[None, :]
     cosine = jnp.concatenate([jnp.cos(angle)] * 2, axis=1)
     sine = jnp.concatenate([-jnp.sin(angle), jnp.sin(angle)], axis=1)
     cot = interleave(cotangent[0, p_len:], cotangent[0, :p_len]).reshape(rows, heads)
@@ -543,7 +572,7 @@
         ),
     )(
         slot, task_of, lengths, interleave(text[0], prompts[0]), gain.reshape(m, 1, width),
-        cosine, sine, pos[:, None], pos[None, :], cot, w_query, w_key, w_value,
+        cosine, sine, jnp.asarray(pos[:, None]), jnp.asarray(pos[None, :]), cot, w_query, w_key, w_value,
     )
     prompt_grad = collected.reshape(n * cp, width)[:p_len][None]
     out = out.reshape(n, chunk, heads)

time: 157 us -> 152 us (0.968)
  Pallas kernels: 145 us -> 141 us
    pallas_call x1, Pallas kernels: 145 us -> 141 us  [fast_device(): pl.pallas_call(functools.partial(step_kernel, p_len), out_shape=(jax.Shap...]
where the time goes in v3:
time: 152 us; the launch traced here: 151 us
  Pallas kernels  141 us (93%)
  local copies, waits for them, and re-layouts  5.43 us (4%)
  other arithmetic  4.47 us (3%)
    pallas_call x1, Pallas kernels, fast_device(): pl.pallas_call(functools.partial(step_kernel, p_len), out_shape=(jax.Shap...  141 us

profile of v3, /device:TPU:11, one launch (start us, length us, event | category | flops | bytes accessed | tf_op | source)
XLA Modules:
  0.0 151.5 jit_solution(13991188341100407334)
XLA Ops:
  0.6 0.0 copy-start.2
  0.7 0.9 slice_bitcast_fusion
  1.6 0.0 copy-start
  1.6 1.0 pad.8
  2.7 1.1 slice.18
  3.8 0.9 pad_maximum_fusion.1
  4.6 0.0 copy-done.2
  4.6 0.8 fusion
  5.4 0.9 pad_maximum_fusion.2
  6.3 0.0 copy-done
  6.3 1.0 pad_maximum_fusion.inp_ref
  7.3 140.9 %shard_map.140 = (bf16[384,768]{1,0:T(8,128)(2,1)}, f32[8,16,1280]{2,1,0:T(8,128)}) custom-call(s32[8]{0:T(128)} %slot_ref.1, s32[8]{0:T(128)} %task_ref.1, s32[8]{0:T(128)} %length_ref.1, bf16[8,48,1280]{2,1,0:T(8,128)(2,1)} %pad_maximum_fusion.inp_ref, f32[4,1,1280]{2,1,0:T(1,128)} %bitcast.26, f32[384,128]{1,0:T(8,128)} %get-tuple-element.9.cos_ref, ...), custom_call_target="tpu_custom_call" | custom-call | tf_op jit(solution)/shard_map/pallas_call | solution.py:537
  148.2 0.0 copy-start.1
  148.2 1.1 slice.27
  149.4 1.1 broadcast_in_dim.9
  150.5 0.0 copy-done.1
  150.6 0.9 maximum_bitcast_fusion
  (5 shorter events, 0.1 us)
Async XLA Ops:
  0.6 4.0 %copy-start.2 = (f32[384]{0:T(512)S(1)}, f32[384]{0:T(512)}, u32[]{:S(2)}) copy-start(f32[384]{0:T(512)} %constant.24) | copy-start | bytes 4612
  1.6 4.7 %copy-start = (bf16[1,256,1280]{2,1,0:T(8,128)(2,1)S(1)}, bf16[1,256,1280]{2,1,0:T(8,128)(2,1)}, u32[]{:S(2)}) copy-start(bf16[1,256,1280]{2,1,0:T(8,128)(2,1)} %param.13) | copy-start | bytes 1966084
  148.2 2.3 %copy-start.1 = (bf16[384,768]{1,0:T(8,128)(2,1)S(1)}, bf16[384,768]{1,0:T(8,128)(2,1)}, u32[]{:S(2)}) copy-start(bf16[384,768]{1,0:T(8,128)(2,1)} %get-tuple-element.4) | copy-start | bytes 1769476
